TPU v7x, 32 devices: a whole 2x2x4 slice. The times are simulated.
32 devices in a mesh: row: 8 (over z, y), col: 4 (over x, core).
Axes of the slice: x: 2, y: 2, z: 4, core: 2. Of those that a mesh axis runs over, the one named last changes fastest.
Arguments:
- matrix_tiles: bfloat16 [8, 4, 96, 256, 256], P('row', 'col'), may hold values from -0.078125 to 0.078125
- tile_rows: int32 [8, 4, 96], P('row', 'col'), may hold values from 0 to 7, as said below
- tile_cols: int32 [8, 4, 96], P('row', 'col'), may hold values from 0 to 15
- tile_count: int32 [8, 4], P('row', 'col'), may hold values from 24 to 96, as said below
- x_start: float32 [16384, 256], P(('col', 'row')), may hold values from -5 to 5
- y_start: float32 [16384, 256], P(('row', 'col')), may hold values from 0 to 1
- cost_vector: float32 [16384, 256], P(('col', 'row')), may hold values from -6 to 6
- right_side: float32 [16384, 256], P(('row', 'col')), may hold values from -6 to 6
- lower_bound: float32 [16384, 256], P(('col', 'row')), may hold values from -1.5 to -0.3
- upper_bound: float32 [16384, 256], P(('col', 'row')), may hold values from 0.3 to 1.5
- step_primal: float32 [256], replicated, may hold values from 0.2 to 0.45
- step_dual: float32 [256], replicated, may hold values from 0.2 to 0.45
Outputs:
- primal_out: float32 [16384, 256], P(('col', 'row'))
- dual_out: float32 [16384, 256], P(('row', 'col'))
Inputs may be any that keep to these rules, and one draw needn't show every extreme that they name: Within one grid cell the pairs (tile_rows, tile_cols) of its slots are all different. `tile_count`: some grid cell has 96 used slots in every draw; slots at or above a cell's count are not part of A.
All inputs are finite; a program needn't handle non-finite values.
Results may differ from a plain program's by a relative error of at most 0.001.
Values may be sent and summed in bfloat16 or wider, within the bound.
A program may use at most 128 MiB of HBM per device.

v0:
```python
import jax
import jax.numpy as jnp
from jax import lax
from jax.sharding import PartitionSpec as P

NR_DEV = 8
SLOT_BLOCK = 16


eps = 1e-06


def forward_part(my_tiles, my_rows, my_cols, slot_count, segment):
    edge = my_tiles.shape[-1]
    batch_width = segment.shape[-1]
    x_tiles = segment.reshape(-1, edge, batch_width)
    slot_ids = jnp.arange(SLOT_BLOCK, dtype=jnp.int32)

    def forward_block_step(block_index, running):
        first_slot = block_index * SLOT_BLOCK
        tile_block = lax.dynamic_slice_in_dim(my_tiles, first_slot, SLOT_BLOCK, 0)
        row_block = lax.dynamic_slice_in_dim(my_rows, first_slot, SLOT_BLOCK, 0)
        col_block = lax.dynamic_slice_in_dim(my_cols, first_slot, SLOT_BLOCK, 0)
        in_use = first_slot + slot_ids < slot_count
        pieces = jnp.take(x_tiles, col_block, axis=0)
        products = jnp.einsum(
            "sij,sjb->sib", tile_block, pieces, preferred_element_type=jnp.float32
        )
        products = jnp.where(in_use[:, None, None], products, jnp.zeros_like(products))
        return running.at[row_block].add(products)

    blocks = (slot_count + SLOT_BLOCK - 1) // SLOT_BLOCK
    begin = jnp.zeros((NR_DEV, edge, batch_width), jnp.float32)
    return lax.fori_loop(0, blocks, forward_block_step, begin).reshape(-1, batch_width)


def backward_part(my_tiles, my_rows, my_cols, slot_count, segment, col_tiles):
    edge = my_tiles.shape[-1]
    batch_width = segment.shape[-1]
    y_tiles = segment.reshape(-1, edge, batch_width)
    slot_ids = jnp.arange(SLOT_BLOCK, dtype=jnp.int32)

    def backward_block_step(block_index, running):
        first_slot = block_index * SLOT_BLOCK
        tile_block = lax.dynamic_slice_in_dim(my_tiles, first_slot, SLOT_BLOCK, 0)
        row_block = lax.dynamic_slice_in_dim(my_rows, first_slot, SLOT_BLOCK, 0)
        col_block = lax.dynamic_slice_in_dim(my_cols, first_slot, SLOT_BLOCK, 0)
        in_use = first_slot + slot_ids < slot_count
        pieces = jnp.take(y_tiles, row_block, axis=0)
        products = jnp.einsum(
            "sij,sib->sjb", tile_block, pieces, preferred_element_type=jnp.float32
        )
        products = jnp.where(in_use[:, None, None], products, jnp.zeros_like(products))
        return running.at[col_block].add(products)

    blocks = (slot_count + SLOT_BLOCK - 1) // SLOT_BLOCK
    begin = jnp.zeros((col_tiles, edge, batch_width), jnp.float32)
    return lax.fori_loop(0, blocks, backward_block_step, begin).reshape(-1, batch_width)


def body(
    matrix_tiles,
    tile_rows,
    tile_cols,
    tile_count,
    x_start,
    y_start,
    cost_vector,
    right_side,
    lower_bound,
    upper_bound,
    step_primal,
    step_dual,
):
    my_tiles = matrix_tiles[0, 0]
    my_rows = tile_rows[0, 0]
    my_cols = tile_cols[0, 0]
    slot_count = tile_count[0, 0]
    row_devices = lax.axis_size("row")
    col_devices = lax.axis_size("col")
    share = x_start.shape[0]
    edge = my_tiles.shape[-1]
    col_tiles = share * row_devices // edge
    total_cols = share * row_devices * col_devices
    total_rows = y_start.shape[0] * row_devices * col_devices

    def dual_rows(values):
        return lax.all_gather(values.astype(jnp.bfloat16), "col", axis=0, tiled=True)

    def row_sums(segment):
        return lax.psum_scatter(
            forward_part(my_tiles, my_rows, my_cols, slot_count, segment),
            "col",
            scatter_dimension=0,
            tiled=True,
        )

    x_base, cost_seg, lower_seg, upper_seg = (x_start, cost_vector, lower_bound, upper_bound)

    def column_sums(segment):
        partial_value = backward_part(my_tiles, my_rows, my_cols, slot_count, segment, col_tiles)
        return lax.psum_scatter(partial_value, "row", scatter_dimension=0, tiled=True)

    def spread(ahead):
        return lax.all_gather(ahead, "row", axis=0, tiled=True)

    grad_zero = column_sums(dual_rows(y_start))
    primal_one = jnp.clip(x_base - step_primal * (cost_seg - grad_zero), lower_seg, upper_seg)
    primal_diff = primal_one - x_base
    move_primal = jnp.sum(primal_diff * primal_diff, axis=0)
    image_one = row_sums(spread((2.0 * primal_one - x_base).astype(jnp.bfloat16)))
    dual_one = jnp.maximum(y_start + step_dual * (right_side - image_one), 0.0)
    dual_diff = dual_one - y_start
    move_dual = jnp.sum(dual_diff * dual_diff, axis=0)
    move_primal, move_dual = lax.psum((move_primal, move_dual), ("row", "col"))
    weight = jnp.sqrt((move_dual / total_rows + eps) / (move_primal / total_cols + eps))
    grad_one = column_sums(dual_rows(dual_one))
    primal_two = jnp.clip(
        primal_one - step_primal / weight * (cost_seg - grad_one), lower_seg, upper_seg
    )
    image_two = row_sums(spread((2.0 * primal_two - primal_one).astype(jnp.bfloat16)))
    dual_out = jnp.maximum(dual_one + step_dual * weight * (right_side - image_two), 0.0)
    return (primal_two, dual_out)


def solution(mesh):
    placed = (
        P("row", "col", None, None, None),
        P("row", "col", None),
        P("row", "col", None),
        P("row", "col"),
        P(("col", "row"), None),
        P(("row", "col"), None),
        P(("col", "row"), None),
        P(("row", "col"), None),
        P(("col", "row"), None),
        P(("col", "row"), None),
        P(),
        P(),
    )
    return jax.shard_map(
        body,
        mesh=mesh,
        in_specs=placed,
        out_specs=(P(("col", "row"), None), P(("row", "col"), None)),
        check_vma=False,
    )
```

profile of v0, /device:TPU:0, one launch (start us, length us, event | category | flops | bytes accessed | tf_op | source)
XLA Modules:
  0.0 776.5 jit_solution(1718431034138353426)
XLA Ops:
  7.2 1.8 convert_element_type.12
  9.7 16.6 %copy.14 = bf16[96,256,256]{1,2,0:T(8,128)(2,1)} copy(bf16[96,256,256]{2,1,0:T(8,128)(2,1)} %bitcast.19) | data formatting | bytes 25165824
  26.4 3.2 all-gather.5.cloned.1.call-done
  29.6 2.4 broadcast.119.clone
  31.9 30.7 %while.44 = (s32[]{:T(128)}, f32[16,256,256]{2,1,0:T(8,128)}, s32[]{:T(128)}, s32[96]{0:T(128)S(1)}, s32[]{:T(128)}, /*index=5*/bf16[96,256,256]{1,2,0:T(8,128)(...) while((s32[]{:T(128)}, f32[16,256,256]{2,1,0:T(8,128)}, ...), condition=%wide.region_2.4_spmd.clone, body=%wide.region_0.3_spmd.clone.sunk | while | flops 540017856 | bytes 25170616 | solution.py:58
  32.0 0.7 compare_and_fusion.8
  32.7 0.7 gather_fusion
  33.4 4.3 convolution_select_fusion.8
  37.7 0.1 compare_select_fusion.16
  37.8 9.5 %scatter_fusion = f32[16,256,256]{2,1,0:T(8,128)} fusion(f32[16,256,256]{2,1,0:T(8,128)} %get-tuple-element.615, s32[16]{0:T(128)S(1)} %compare_select_fusion.16, f32[16,256,256]{2,1,0:T(8,128)} %convolution_select_fusion.8), kind=kCustom, calls=%fused_computation.4.clone.clone.1 | custom fusion | flops 1048576 | bytes 12582976 | tf_op jit(solution)/shard_map/while/body/scatter-add | solution.py:54
  47.2 0.7 compare_and_fusion.8
  48.0 0.7 gather_fusion
  48.7 4.3 convolution_select_fusion.8
  53.0 0.1 compare_select_fusion.16
  53.1 9.5 %scatter_fusion = f32[16,256,256]{2,1,0:T(8,128)} fusion(f32[16,256,256]{2,1,0:T(8,128)} %get-tuple-element.615, s32[16]{0:T(128)S(1)} %compare_select_fusion.16, f32[16,256,256]{2,1,0:T(8,128)} %convolution_select_fusion.8), kind=kCustom, calls=%fused_computation.4.clone.clone.1 | custom fusion | flops 1048576 | bytes 12582976 | tf_op jit(solution)/shard_map/while/body/scatter-add | solution.py:54
  62.7 149.1 %reduce-scatter.5.cloned.1.call-done = f32[512,256]{1,0:T(8,128)} async-done(((f32[4096,256]{1,0:T(8,128)}), f32[512,256]{1,0:T(8,128)}) %reduce-scatter.5.cloned.1.call-update) | async-done | bytes 524304 | tf_op jit(solution)/shard_map/reduce_scatter | solution.py:102
  211.9 1.2 multiply_reduce_fusion
  213.1 0.8 copy-done.6
  213.9 0.8 subtract_convert_fusion.1
  214.7 48.8 %all-gather.7.cloned.1.call-done = bf16[4096,256]{1,0:T(8,128)(2,1)} async-done(((bf16[512,256]{1,0:T(8,128)(2,1)}), bf16[4096,256]{1,0:T(8,128)(2,1)}) %all-gather.7.cloned.1.call-update) | async-done | bytes 2097168 | tf_op jit(solution)/shard_map/all_gather | solution.py:105
  263.6 0.2 broadcast.120.clone
  263.8 31.0 %while.45 = (s32[]{:T(128)}, f32[8,256,256]{2,1,0:T(8,128)S(1)}, s32[]{:T(128)}, s32[96]{0:T(128)S(1)}, s32[]{:T(128)}, /*index=5*/bf16[96,256,256]{2,1,0:T(8,12...) while((s32[]{:T(128)}, f32[8,256,256]{2,1,0:T(8,128)S(1)}, ...), condition=%wide.region_6.9_spmd.clone, body=%wide.region_4.8_spmd.clone.sunk | while | flops 540017856 | bytes 25170616 | solution.py:34
  263.8 0.7 compare_and_fusion.9
  264.5 3.6 gather_fusion.1
  268.1 5.0 convolution_select_fusion.9
  273.1 6.1 scatter_fusion.1
  279.3 0.7 compare_and_fusion.9
  280.0 3.6 gather_fusion.1
  283.6 4.9 convolution_select_fusion.9
  288.6 6.1 scatter_fusion.1
  294.8 1.3 copy-done.1
  296.2 91.9 %reduce-scatter.7.cloned.1.call-done = f32[512,256]{1,0:T(8,128)} async-done(((f32[2048,256]{1,0:T(8,128)}), f32[512,256]{1,0:T(8,128)}) %reduce-scatter.7.cloned.1.call-update) | async-done | bytes 524304 | tf_op jit(solution)/shard_map/reduce_scatter | solution.py:91
  388.1 1.2 multiply_reduce_fusion.1
  389.3 0.8 copy-done.4
  390.1 0.7 convert_element_type.14
  390.9 16.8 %all-gather.9.cloned.1.call-done = bf16[2048,256]{1,0:T(8,128)(2,1)} async-done(((bf16[512,256]{1,0:T(8,128)(2,1)}), bf16[2048,256]{1,0:T(8,128)(2,1)}) %all-gather.9.cloned.1.call-update) | async-done | bytes 1048592 | tf_op jit(solution)/shard_map/all_gather | solution.py:88
  407.7 2.4 broadcast.119
  410.1 30.7 %while.46 = (s32[]{:T(128)}, f32[16,256,256]{2,1,0:T(8,128)}, s32[]{:T(128)}, s32[96]{0:T(128)S(1)}, s32[]{:T(128)}, /*index=5*/bf16[96,256,256]{1,2,0:T(8,128)(...) while((s32[]{:T(128)}, f32[16,256,256]{2,1,0:T(8,128)}, ...), condition=%wide.region_14.17_spmd.clone, body=%wide.region_12.16_spmd.clone.sunk | while | flops 540017856 | bytes 25170616 | solution.py:58
  410.1 0.7 compare_and_fusion.10
  410.8 0.7 gather_fusion.2
  411.5 4.3 convolution_select_fusion.10
  415.8 0.1 compare_select_fusion.18
  415.9 9.5 %scatter_fusion.2 = f32[16,256,256]{2,1,0:T(8,128)} fusion(f32[16,256,256]{2,1,0:T(8,128)} %get-tuple-element.687, s32[16]{0:T(128)S(1)} %compare_select_fusion.18, f32[16,256,256]{2,1,0:T(8,128)} %convolution_select_fusion.10), kind=kCustom, calls=%fused_computation.6.clone.clone.1 | custom fusion | flops 1048576 | bytes 12582976 | tf_op jit(solution)/shard_map/while/body/scatter-add | solution.py:54
  425.4 0.7 compare_and_fusion.10
  426.1 0.7 gather_fusion.2
  426.8 4.3 convolution_select_fusion.10
  431.2 9.6 %scatter_fusion.2 = f32[16,256,256]{2,1,0:T(8,128)} fusion(f32[16,256,256]{2,1,0:T(8,128)} %get-tuple-element.687, s32[16]{0:T(128)S(1)} %compare_select_fusion.18, f32[16,256,256]{2,1,0:T(8,128)} %convolution_select_fusion.10), kind=kCustom, calls=%fused_computation.6.clone.clone.1 | custom fusion | flops 1048576 | bytes 12582976 | tf_op jit(solution)/shard_map/while/body/scatter-add | solution.py:54
  440.8 103.1 %all-reduce = (f32[256]{0:T(256)S(1)}, f32[256]{0:T(256)S(1)}) all-reduce(f32[256]{0:T(256)S(1)} %get-tuple-element.372, f32[256]{0:T(256)S(1)} %get-tuple-element.370), channel_id=1, replica_groups=mesh['row'=8,'col'=4] {'row','col'}, use_global_device_ids=true, to_apply=%region_11.14 | all-reduce | flops 512 | bytes 4096 | tf_op jit(solution)/shard_map/psum | solution.py:115
  543.9 47.3 %reduce-scatter.9.cloned.1.call-done = f32[512,256]{1,0:T(8,128)} async-done(((f32[4096,256]{1,0:T(8,128)}), f32[512,256]{1,0:T(8,128)}) %reduce-scatter.9.cloned.1.call-update) | async-done | bytes 524304 | tf_op jit(solution)/shard_map/reduce_scatter | solution.py:102
  591.2 2.1 subtract_convert_fusion
  593.4 49.3 %all-gather.11.cloned.1.call-done = bf16[4096,256]{1,0:T(8,128)(2,1)} async-done(((bf16[512,256]{1,0:T(8,128)(2,1)}), bf16[4096,256]{1,0:T(8,128)(2,1)}) %all-gather.11.cloned.1.call-update) | async-done | bytes 2097168 | tf_op jit(solution)/shard_map/all_gather | solution.py:105
  642.7 0.2 broadcast.120
  642.9 31.2 %while.47 = (s32[]{:T(128)}, f32[8,256,256]{2,1,0:T(8,128)S(1)}, s32[]{:T(128)}, s32[96]{0:T(128)S(1)}, s32[]{:T(128)}, /*index=5*/bf16[96,256,256]{2,1,0:T(8,12...) while((s32[]{:T(128)}, f32[8,256,256]{2,1,0:T(8,128)S(1)}, ...), condition=%wide.region_18.21_spmd.clone, body=%wide.region_16.20_spmd.clone.sunk | while | flops 540017856 | bytes 25170616 | solution.py:34
  642.9 0.7 compare_and_fusion.11
  643.6 3.7 gather_fusion.3
  647.3 5.0 convolution_select_fusion.11
  652.3 6.1 scatter_fusion.3
  658.5 0.7 compare_and_fusion.11
  659.2 3.7 gather_fusion.3
  662.9 5.0 convolution_select_fusion.11
  667.9 6.1 scatter_fusion.3
  674.1 1.3 copy-done
  675.4 92.3 %reduce-scatter.11.cloned.1.call-done = f32[512,256]{1,0:T(8,128)} async-done(((f32[2048,256]{1,0:T(8,128)}), f32[512,256]{1,0:T(8,128)}) %reduce-scatter.11.cloned.1.call-update) | async-done | bytes 524304 | tf_op jit(solution)/shard_map/reduce_scatter | solution.py:91
  767.8 1.9 add_maximum_fusion
  (71 shorter events, 1.0 us)
Async XLA Ops:
  7.2 22.4 %all-gather.5.cloned.1.call-start = ((), (), s32[]{:S(2)}) async-start(), calls=%async_computation.4 | async-start | bytes 1310720 | tf_op jit(solution)/shard_map/all_gather | solution.py:88
  9.0 202.9 %reduce-scatter.5.cloned.1.call-start = ((), (), s32[]{:S(2)}) async-start(), calls=%async_computation.5 | async-start | bytes 4718592 | tf_op jit(solution)/shard_map/reduce_scatter | solution.py:102
  29.6 2.4 copy-start.2
  29.6 2.4 copy-start.18
  29.6 2.4 copy-start.19
  62.6 149.2 %copy-start.9 = (f32[512,256]{1,0:T(8,128)S(1)}, f32[512,256]{1,0:T(8,128)}, u32[]{:S(2)}) copy-start(f32[512,256]{1,0:T(8,128)} %param.33) | copy-start | bytes 1572868
  62.6 149.2 %copy-start.11 = (f32[512,256]{1,0:T(8,128)S(1)}, f32[512,256]{1,0:T(8,128)}, u32[]{:S(2)}) copy-start(f32[512,256]{1,0:T(8,128)} %param.32) | copy-start | bytes 1572868
  62.6 149.2 %copy-start.13 = (f32[512,256]{1,0:T(8,128)S(1)}, f32[512,256]{1,0:T(8,128)}, u32[]{:S(2)}) copy-start(f32[512,256]{1,0:T(8,128)} %param.30) | copy-start | bytes 1572868
  62.6 149.2 %copy-start.17 = (f32[512,256]{1,0:T(8,128)S(1)}, f32[512,256]{1,0:T(8,128)}, u32[]{:S(2)}) copy-start(f32[512,256]{1,0:T(8,128)} %param.28) | copy-start | bytes 1572868
  62.6 149.2 %copy-start.21 = (f32[256]{0:T(256)S(1)}, f32[256]{0:T(256)}, u32[]{:S(2)}) copy-start(f32[256]{0:T(256)} %param.34) | copy-start | bytes 3076
  62.7 200.9 %all-gather.7.cloned.1.call-start = ((), (), s32[]{:S(2)}) async-start(), calls=%async_computation.6 | async-start | bytes 2359296 | tf_op jit(solution)/shard_map/all_gather | solution.py:105
  213.1 0.8 copy-start.6
  214.7 173.4 %reduce-scatter.7.cloned.1.call-start = ((), (), s32[]{:S(2)}) async-start(), calls=%async_computation.7 | async-start | bytes 2621440 | tf_op jit(solution)/shard_map/reduce_scatter | solution.py:91
  294.8 1.3 copy-start.1
  294.8 93.3 %copy-start.8 = (f32[512,256]{1,0:T(8,128)S(1)}, f32[512,256]{1,0:T(8,128)}, u32[]{:S(2)}) copy-start(f32[512,256]{1,0:T(8,128)} %param.29) | copy-start | bytes 1572868
  294.8 93.3 %copy-start.15 = (f32[512,256]{1,0:T(8,128)S(1)}, f32[512,256]{1,0:T(8,128)}, u32[]{:S(2)}) copy-start(f32[512,256]{1,0:T(8,128)} %param.31) | copy-start | bytes 1572868
  294.8 93.3 %copy-start.20 = (f32[256]{0:T(256)S(1)}, f32[256]{0:T(256)}, u32[]{:S(2)}) copy-start(f32[256]{0:T(256)} %param.35) | copy-start | bytes 3076
  296.1 111.6 %all-gather.9.cloned.1.call-start = ((), (), s32[]{:S(2)}) async-start(), calls=%async_computation.8 | async-start | bytes 1310720 | tf_op jit(solution)/shard_map/all_gather | solution.py:88
  389.3 0.8 copy-start.4
  390.8 200.4 %reduce-scatter.9.cloned.1.call-start = ((), (), s32[]{:S(2)}) async-start(), calls=%async_computation.9 | async-start | bytes 4718592 | tf_op jit(solution)/shard_map/reduce_scatter | solution.py:102
  407.7 2.4 copy-start.3
  440.8 150.5 %copy-start.7 = (f32[512,256]{1,0:T(8,128)S(1)}, f32[512,256]{1,0:T(8,128)}, u32[]{:S(2)}) copy-start(f32[512,256]{1,0:T(8,128)} %copy-done.6) | copy-start | bytes 1572868
  440.8 150.5 %copy-start.10 = (f32[512,256]{1,0:T(8,128)S(1)}, f32[512,256]{1,0:T(8,128)}, u32[]{:S(2)}) copy-start(f32[512,256]{1,0:T(8,128)} %param.33) | copy-start | bytes 1572868
  440.8 150.5 %copy-start.12 = (f32[512,256]{1,0:T(8,128)S(1)}, f32[512,256]{1,0:T(8,128)}, u32[]{:S(2)}) copy-start(f32[512,256]{1,0:T(8,128)} %param.32) | copy-start | bytes 1572868
  440.8 150.5 %copy-start.14 = (f32[512,256]{1,0:T(8,128)S(1)}, f32[512,256]{1,0:T(8,128)}, u32[]{:S(2)}) copy-start(f32[512,256]{1,0:T(8,128)} %param.30) | copy-start | bytes 1572868
  440.8 201.9 %all-gather.11.cloned.1.call-start = ((), (), s32[]{:S(2)}) async-start(), calls=%async_computation.10 | async-start | bytes 2359296 | tf_op jit(solution)/shard_map/all_gather | solution.py:105
  593.4 174.4 %reduce-scatter.11.cloned.1.call-start = ((), (), s32[]{:S(2)}) async-start(), calls=%async_computation.11 | async-start | bytes 2621440 | tf_op jit(solution)/shard_map/reduce_scatter | solution.py:91
  674.1 1.3 copy-start
  674.1 93.7 %copy-start.5 = (f32[512,256]{1,0:T(8,128)S(1)}, f32[512,256]{1,0:T(8,128)}, u32[]{:S(2)}) copy-start(f32[512,256]{1,0:T(8,128)} %copy-done.4) | copy-start | bytes 1572868
  674.1 93.7 %copy-start.16 = (f32[512,256]{1,0:T(8,128)S(1)}, f32[512,256]{1,0:T(8,128)}, u32[]{:S(2)}) copy-start(f32[512,256]{1,0:T(8,128)} %param.31) | copy-start | bytes 1572868
Sparse Core Ops, SparseCore 0:
  10.1 19.4 all-gather.4
  62.8 149.0 reduce-scatter.4
  214.8 48.7 all-gather.6
  296.2 91.7 reduce-scatter.6
  390.9 16.6 all-gather.8
  440.9 150.2 reduce-scatter.8
  593.9 48.6 all-gather.10
  675.6 92.1 reduce-scatter.10
where the time goes:
time: 780 us; the launch traced here: 777 us
  waiting for transfers between devices  499 us (64%)
  blocking collectives  103 us (13%)
  other arithmetic  78.8 us (10%)
  local copies, waits for them, and re-layouts  43.2 us (6%)
  matrix products  37.1 us (5%)
  between operations  15 us (2%)
    reduce_scatter x2, waiting for transfers between devices, column_sums(): lax.psum_scatter(partial_value, 'row', scatter_dimension=0, tiled=True)  196 us
    reduce_scatter x2, waiting for transfers between devices, row_sums(): lax.psum_scatter(forward_part(my_tiles, my_rows, my_cols, slot_count, seg...  184 us
    psum x1, blocking collectives, body(): move_primal, move_dual = lax.psum((move_primal, move_dual), ('row', 'col'))  103 us
    all_gather x2, waiting for transfers between devices, spread(): return lax.all_gather(ahead, 'row', axis=0, tiled=True)  98.1 us
    scatter-add x4, other arithmetic, backward_block_step(): return running.at[col_block].add(products)  38 us
    scatter-add x4, other arithmetic, forward_block_step(): return running.at[row_block].add(products)  24.6 us
    unnamed x45, local copies, waits for them, and re-layouts  20.9 us
    all_gather x2, waiting for transfers between devices, dual_rows(): lax.all_gather(values.astype(jnp.bfloat16), 'col', axis=0, tiled=True)  20 us
  transfers between devices with their start and end apart: 8, of which 8 were waited for; matrix products, arithmetic and copies ran while one was open for 2% of the time, Pallas kernels for 0%

commit v1 on v0

v1 whole, which is shorter than its diff:
```python
import jax
import jax.numpy as jnp
from jax import lax
from jax.experimental import pallas as pl
from jax.experimental.pallas import tpu as pltpu
from jax.sharding import PartitionSpec as P

NR_DEV = 8
ZERO_ROWS = 16

eps = 1e-06


def lay_out_kernel(count_ref, rows_ref, cols_ref, tiles_ref, dense_ref, sems):
    edge = tiles_ref.shape[-1]
    count = count_ref[0, 0]

    @pl.loop(0, dense_ref.shape[0] // ZERO_ROWS)
    def _(step):
        at = pl.ds(pl.multiple_of(step * ZERO_ROWS, ZERO_ROWS), ZERO_ROWS)
        dense_ref[at, :] = jnp.zeros((ZERO_ROWS, dense_ref.shape[1]), dense_ref.dtype)

    def copy_of(slot):
        first_row = pl.multiple_of(rows_ref[0, 0, slot] * edge, edge)
        first_col = pl.multiple_of(cols_ref[0, 0, slot] * edge, edge)
        return pltpu.make_async_copy(
            tiles_ref.at[0, 0, slot],
            dense_ref.at[pl.ds(first_row, edge), pl.ds(first_col, edge)],
            sems.at[slot],
        )

    @pl.loop(0, count)
    def _(slot):
        copy_of(slot).start()

    @pl.loop(0, count)
    def _(slot):
        copy_of(slot).wait()


def lay_out(matrix_tiles, tile_rows, tile_cols, tile_count, col_tiles):
    slots, edge = matrix_tiles.shape[2], matrix_tiles.shape[-1]
    shape = (NR_DEV * edge, col_tiles * edge)
    return pl.pallas_call(
        lay_out_kernel,
        out_shape=jax.ShapeDtypeStruct(shape, matrix_tiles.dtype),
        in_specs=[pl.BlockSpec(memory_space=pltpu.SMEM)] * 3
        + [pl.BlockSpec(memory_space=pl.ANY)],
        out_specs=pl.BlockSpec(memory_space=pltpu.VMEM),
        scratch_shapes=[pltpu.SemaphoreType.DMA((slots,))],
        compiler_params=pltpu.CompilerParams(vmem_limit_bytes=40 << 20),
        cost_estimate=pl.CostEstimate(
            flops=0, bytes_accessed=2 * shape[0] * shape[1] * 2, transcendentals=0
        ),
        name="lay_out",
    )(tile_count, tile_rows, tile_cols, matrix_tiles)


def exchange_sum(partial, axis):
    pieces = partial.astype(jnp.bfloat16).reshape(lax.axis_size(axis), -1, partial.shape[-1])
    arrived = lax.all_to_all(pieces, axis, split_axis=0, concat_axis=0, tiled=True)
    return jnp.sum(arrived.astype(jnp.float32), axis=0)


def body(
    matrix_tiles,
    tile_rows,
    tile_cols,
    tile_count,
    x_start,
    y_start,
    cost_seg,
    right_side,
    lower_seg,
    upper_seg,
    step_primal,
    step_dual,
):
    row_devices = lax.axis_size("row")
    col_devices = lax.axis_size("col")
    share = x_start.shape[0]
    edge = matrix_tiles.shape[-1]
    col_tiles = share * row_devices // edge
    total_cols = share * row_devices * col_devices
    total_rows = y_start.shape[0] * row_devices * col_devices
    dense = lay_out(matrix_tiles, tile_rows, tile_cols, tile_count, col_tiles)

    def column_sums(dual):
        segment = lax.all_gather(dual.astype(jnp.bfloat16), "col", axis=0, tiled=True)
        partial = lax.dot_general(
            dense, segment, (((0,), (0,)), ((), ())), preferred_element_type=jnp.float32
        )
        return exchange_sum(partial, "row")

    def row_sums(ahead):
        segment = lax.all_gather(ahead.astype(jnp.bfloat16), "row", axis=0, tiled=True)
        partial = jnp.dot(dense, segment, preferred_element_type=jnp.float32)
        return exchange_sum(partial, "col")

    grad_zero = column_sums(y_start)
    primal_one = jnp.clip(x_start - step_primal * (cost_seg - grad_zero), lower_seg, upper_seg)
    primal_diff = primal_one - x_start
    move_primal = jnp.sum(primal_diff * primal_diff, axis=0)
    image_one = row_sums(2.0 * primal_one - x_start)
    dual_one = jnp.maximum(y_start + step_dual * (right_side - image_one), 0.0)
    dual_diff = dual_one - y_start
    move_dual = jnp.sum(dual_diff * dual_diff, axis=0)
    moves = lax.psum(jnp.stack([move_primal, move_dual]), ("row", "col"))
    weight = jnp.sqrt((moves[1] / total_rows + eps) / (moves[0] / total_cols + eps))
    grad_one = column_sums(dual_one)
    primal_two = jnp.clip(
        primal_one - step_primal / weight * (cost_seg - grad_one), lower_seg, upper_seg
    )
    image_two = row_sums(2.0 * primal_two - primal_one)
    dual_out = jnp.maximum(dual_one + step_dual * weight * (right_side - image_two), 0.0)
    return (primal_two, dual_out)


def solution(mesh):
    placed = (
        P("row", "col", None, None, None),
        P("row", "col", None),
        P("row", "col", None),
        P("row", "col"),
        P(("col", "row"), None),
        P(("row", "col"), None),
        P(("col", "row"), None),
        P(("row", "col"), None),
        P(("col", "row"), None),
        P(("col", "row"), None),
        P(),
        P(),
    )
    return jax.shard_map(
        body,
        mesh=mesh,
        in_specs=placed,
        out_specs=(P(("col", "row"), None), P(("row", "col"), None)),
        check_vma=False,
    )
```

time: 780 us -> 363 us (0.47)
  waiting for transfers between devices: 499 us -> 116 us
  other arithmetic: 78.8 us -> 6.46 us
  blocking collectives: 103 us -> 157 us
  local copies, waits for them, and re-layouts: 43.2 us -> 8.16 us
  Pallas kernels: 0 us -> 9.41 us
  matrix products: 37.1 us -> 45.4 us
    reduce_scatter x4 -> x0, waiting for transfers between devices: 381 us -> none  [the longest x2 196 us: column_sums(): lax.psum_scatter(partial_value, 'row', scatter_dimension=0, tiled=True)]
    all_to_all x0 -> x3, blocking collectives: none -> 88.1 us  [exchange_sum(): lax.all_to_all(pieces, axis, split_axis=0, concat_axis=0, tiled=True)]
    scatter-add x8 -> x0, other arithmetic: 62.6 us -> none  [the longest x4 38 us: backward_block_step(): return running.at[col_block].add(products)]
    psum x1, blocking collectives: 103 us -> 68.7 us  [body(): moves = lax.psum(jnp.stack([move_primal, move_dual]), ('row', 'col'))]
    gather x8 -> x0, local copies, waits for them, and re-layouts: 17.2 us -> none  [the longest x4 14.5 us: forward_block_step(): pieces = jnp.take(x_tiles, col_block, axis=0)]
    unnamed x45 -> x30, local copies, waits for them, and re-layouts: 20.9 us -> 8.16 us
    pallas_call x0 -> x1, Pallas kernels: none -> 9.41 us  [lay_out(): pl.pallas_call(lay_out_kernel, out_shape=jax.ShapeDtypeStruct(shape, matr...]
    dot_general x8 -> x4, matrix products: 37.1 us -> 45.4 us  [the longest x2 23.3 us: column_sums(): lax.dot_general(dense, segment, (((0,), (0,)), ((), ())), preferred_eleme...]
  transfers between devices with their start and end apart: 8 -> 5, of which waited for: 8 -> 4; matrix products, arithmetic and copies ran while one was open for 2% -> 0% of each run, Pallas kernels for 0% -> 3%
where the time goes in v1:
time: 363 us; the launch traced here: 362 us
  blocking collectives  157 us (43%)
  waiting for transfers between devices  116 us (32%)
  matrix products  45.4 us (13%)
  between operations  14.6 us (4%)
  Pallas kernels  9.41 us (3%)
  local copies, waits for them, and re-layouts  8.16 us (2%)
  other arithmetic  6.46 us (2%)
  starting transfers between devices  5.67 us (2%)
    all_gather x2, waiting for transfers between devices, row_sums(): lax.all_gather(ahead.astype(jnp.bfloat16), 'row', axis=0, tiled=True)  96.4 us
    all_to_all x3, blocking collectives, exchange_sum(): lax.all_to_all(pieces, axis, split_axis=0, concat_axis=0, tiled=True)  88.1 us
    psum x1, blocking collectives, body(): moves = lax.psum(jnp.stack([move_primal, move_dual]), ('row', 'col'))  68.7 us
    dot_general x2, matrix products, column_sums(): lax.dot_general(dense, segment, (((0,), (0,)), ((), ())), preferred_eleme...  23.3 us
    dot_general x2, matrix products, row_sums(): partial = jnp.dot(dense, segment, preferred_element_type=jnp.float32)  22.1 us
    all_gather x2, waiting for transfers between devices, column_sums(): lax.all_gather(dual.astype(jnp.bfloat16), 'col', axis=0, tiled=True)  19 us
    pallas_call x1, Pallas kernels, lay_out(): pl.pallas_call(lay_out_kernel, out_shape=jax.ShapeDtypeStruct(shape, matr...  9.41 us
    unnamed x30, local copies, waits for them, and re-layouts  8.16 us
  transfers between devices with their start and end apart: 5, of which 4 were waited for; matrix products, arithmetic and copies ran while one was open for 0% of the time, Pallas kernels for 3%

profile of v1, /device:TPU:0, one launch (start us, length us, event | category | flops | bytes accessed | tf_op | source)
XLA Modules:
  0.0 362.1 jit_solution(10805689634496363579)
XLA Ops:
  7.2 0.0 all-gather.5.cloned.1.call-start
  7.2 1.8 convert_element_type.36
  9.0 0.0 all-gather.5.cloned.1.call-update
  9.0 0.0 all-gather.7.cloned.1.call-start
  9.7 0.0 copy-start
  9.7 4.6 %copy-done = bf16[1,1,96,256,256]{4,3,2,1,0:T(8,128)(2,1)S(1)} copy-done((bf16[1,1,96,256,256]{4,3,2,1,0:T(8,128)(2,1)S(1)}, bf16[1,1,96,256,256]{4,3,2,1,0:T(8,128)(2,1)}, u32[]{:S(2)}) %copy-start) | copy-done | bytes 12582936
  14.3 0.0 copy-start.1
  14.3 0.7 copy-done.1
  14.9 0.0 copy-start.2
  14.9 0.7 copy-done.2
  15.6 9.4 %lay_out.1 = bf16[2048,4096]{1,0:T(8,128)(2,1)} custom-call(s32[1,1]{1,0:T(1,128)S(6)} %copy.14.count_ref, s32[1,1,96]{2,1,0:T(1,128)S(1)} %copy-done.1, s32[1,1,96]{2,1,0:T(1,128)S(1)} %copy-done.2, bf16[1,1,96,256,256]{4,3,2,1,0:T(8,128)(2,1)S(1)} %copy-done), custom_call_target="tpu_custom_call" | custom-call | bytes 33554432 | tf_op jit(solution)/shard_map/lay_out/pallas_call | solution.py:44
  25.0 4.6 %all-gather.5.cloned.1.call-done = bf16[2048,256]{1,0:T(8,128)(2,1)} async-done(((bf16[512,256]{1,0:T(8,128)(2,1)}), bf16[2048,256]{1,0:T(8,128)(2,1)}) %all-gather.5.cloned.1.call-update) | async-done | bytes 1048592 | tf_op jit(solution)/shard_map/all_gather | solution.py:89
  29.6 11.0 %convolution_convert_fusion.1 = bf16[4096,256]{1,0:T(8,128)(2,1)S(1)} fusion(bf16[2048,4096]{1,0:T(8,128)(2,1)} %lay_out.1, bf16[2048,256]{1,0:T(8,128)(2,1)} %all-gather.5.cloned.1.call-done), kind=kOutput, calls=%fused_computation.1 | convolution fusion | flops 4296015872 | bytes 19922944 | tf_op jit(solution)/shard_map/dot_general | solution.py:90
  40.6 53.9 %all_to_all.20 = bf16[8,512,256]{2,1,0:T(8,128)(2,1)S(1)} all-to-all(bf16[8,512,256]{2,1,0:T(8,128)(2,1)S(1)} %bitcast.16), channel_id=1, replica_groups=mesh['row'=8,'col'=4] {'row'}, dimensions={0} | all-to-all | bytes 4194304 | tf_op jit(solution)/shard_map/all_to_all | solution.py:61
  94.5 0.0 copy-start.4
  94.5 0.0 copy-start.6
  94.5 0.0 copy-start.8
  94.5 0.0 copy-start.12
  94.5 0.0 copy-start.14
  94.5 0.3 convert_reduce_fusion.1
  94.8 0.7 copy-done.4
  95.5 0.2 copy-done.6
  95.7 0.2 copy-done.8
  95.8 0.2 copy-done.12
  96.0 0.0 copy-done.14
  96.0 0.2 multiply_reduce_fusion.1
  96.2 0.8 subtract_convert_fusion.1
  96.9 0.0 all-gather.7.cloned.1.call-update
  97.0 0.0 all-gather.9.cloned.1.call-start
  97.0 47.3 %all-gather.7.cloned.1.call-done = bf16[4096,256]{1,0:T(8,128)(2,1)} async-done(((bf16[512,256]{1,0:T(8,128)(2,1)}), bf16[4096,256]{1,0:T(8,128)(2,1)}) %all-gather.7.cloned.1.call-update) | async-done | bytes 2097168 | tf_op jit(solution)/shard_map/all_gather | solution.py:96
  144.3 11.1 %convolution_convert_fusion.3 = bf16[2048,256]{1,0:T(8,128)(2,1)S(1)} fusion(bf16[2048,4096]{1,0:T(8,128)(2,1)} %lay_out.1, bf16[4096,256]{1,0:T(8,128)(2,1)} %all-gather.7.cloned.1.call-done), kind=kOutput, calls=%fused_computation.5 | convolution fusion | flops 4295491584 | bytes 19922944 | tf_op jit(solution)/shard_map/dot_general | solution.py:97
  155.4 0.0 copy-start.3
  155.4 0.0 copy-start.10
  155.4 0.0 copy-start.13
  155.4 17.1 %all_to_all.21 = bf16[4,512,256]{2,1,0:T(8,128)(2,1)S(1)} all-to-all(bf16[4,512,256]{2,1,0:T(8,128)(2,1)S(1)} %bitcast.18), channel_id=1, replica_groups=mesh['row'=8,'col'=4] {'col'}, dimensions={0} | all-to-all | bytes 2097152 | tf_op jit(solution)/shard_map/all_to_all | solution.py:61
  172.5 0.1 convert_reduce_fusion.3
  172.7 0.0 copy-done.3
  172.7 0.0 copy-done.10
  172.7 0.0 copy-done.13
  172.7 0.1 multiply_reduce_fusion
  172.9 0.7 convert_element_type.42
  173.6 0.0 all-gather.9.cloned.1.call-update
  173.6 14.5 %all-gather.9.cloned.1.call-done = bf16[2048,256]{1,0:T(8,128)(2,1)} async-done(((bf16[512,256]{1,0:T(8,128)(2,1)}), bf16[2048,256]{1,0:T(8,128)(2,1)}) %all-gather.9.cloned.1.call-update) | async-done | bytes 1048592 | tf_op jit(solution)/shard_map/all_gather | solution.py:89
  188.1 12.3 %convolution_convert_fusion = bf16[4096,256]{1,0:T(8,128)(2,1)} fusion(bf16[2048,4096]{1,0:T(8,128)(2,1)} %lay_out.1, bf16[2048,256]{1,0:T(8,128)(2,1)} %all-gather.9.cloned.1.call-done), kind=kOutput, calls=%fused_computation | convolution fusion | flops 4296015872 | bytes 19922944 | tf_op jit(solution)/shard_map/dot_general | solution.py:90
  200.4 5.5 %all-to-all-start.2 = ((bf16[8,512,256]{2,1,0:T(8,128)(2,1)}), bf16[8,512,256]{2,1,0:T(8,128)(2,1)S(1)}, u32[]{:S(2)}, u32[]{:S(2)}) async-start(bf16[8,512,256]{2,1,0:T(8,128)(2,1)} %bitcast.15), calls=%async_computation.2 | async-start | bytes 4194304 | tf_op jit(solution)/shard_map/all_to_all | solution.py:61
  205.9 0.0 all-gather.11.cloned.1.call-start
  206.0 68.7 %psum.7 = f32[2,256]{1,0:T(2,128)S(1)} all-reduce(f32[2,256]{1,0:T(2,128)S(1)} %pad_maximum_fusion), channel_id=1, replica_groups=mesh['row'=8,'col'=4] {'row','col'}, use_global_device_ids=true, to_apply=%region_4.5 | all-reduce | flops 512 | bytes 4096 | tf_op jit(solution)/shard_map/psum | solution.py:108
  274.7 0.0 all-to-all-done.2
  274.7 0.0 copy-start.5
  274.7 0.0 copy-start.7
  274.8 0.0 copy-start.9
  274.8 0.3 convert_reduce_fusion
  275.1 0.7 copy-done.5
  275.8 0.2 copy-done.7
  275.9 0.2 copy-done.9
  276.1 1.1 subtract_convert_fusion
  277.1 0.0 all-gather.11.cloned.1.call-update
  277.2 49.1 %all-gather.11.cloned.1.call-done = bf16[4096,256]{1,0:T(8,128)(2,1)} async-done(((bf16[512,256]{1,0:T(8,128)(2,1)}), bf16[4096,256]{1,0:T(8,128)(2,1)}) %all-gather.11.cloned.1.call-update) | async-done | bytes 2097168 | tf_op jit(solution)/shard_map/all_gather | solution.py:96
  326.3 11.1 %convolution_convert_fusion.2 = bf16[2048,256]{1,0:T(8,128)(2,1)S(1)} fusion(bf16[2048,4096]{1,0:T(8,128)(2,1)} %lay_out.1, bf16[4096,256]{1,0:T(8,128)(2,1)} %all-gather.11.cloned.1.call-done), kind=kOutput, calls=%fused_computation.4 | convolution fusion | flops 4295491584 | bytes 19922944 | tf_op jit(solution)/shard_map/dot_general | solution.py:97
  337.4 0.0 copy-start.11
  337.4 17.1 %all_to_all.22 = bf16[4,512,256]{2,1,0:T(8,128)(2,1)S(1)} all-to-all(bf16[4,512,256]{2,1,0:T(8,128)(2,1)S(1)} %bitcast.17), channel_id=1, replica_groups=mesh['row'=8,'col'=4] {'col'}, dimensions={0} | all-to-all | bytes 2097152 | tf_op jit(solution)/shard_map/all_to_all | solution.py:61
  354.5 0.1 convert_reduce_fusion.2
  354.6 0.0 copy-done.11
  354.6 0.9 add_maximum_fusion
  (3 shorter events, 0.0 us)
Async XLA Ops:
  7.2 22.4 %all-gather.5.cloned.1.call-start = ((), (), s32[]{:S(2)}) async-start(), calls=%async_computation.4 | async-start | bytes 1310720 | tf_op jit(solution)/shard_map/all_gather | solution.py:89
  9.0 135.3 %all-gather.7.cloned.1.call-start = ((), (), s32[]{:S(2)}) async-start(), calls=%async_computation.5 | async-start | bytes 2359296 | tf_op jit(solution)/shard_map/all_gather | solution.py:96
  9.7 4.6 %copy-start = (bf16[1,1,96,256,256]{4,3,2,1,0:T(8,128)(2,1)S(1)}, bf16[1,1,96,256,256]{4,3,2,1,0:T(8,128)(2,1)}, u32[]{:S(2)}) copy-start(bf16[1,1,96,256,256]{4,3,2,1,0:T(8,128)(2,1)} %tiles_ref.1) | copy-start | bytes 37748740
  14.3 0.7 copy-start.1
  14.9 0.7 copy-start.2
  94.5 1.0 copy-start.4
  94.5 1.2 copy-start.6
  94.5 1.4 copy-start.8
  94.5 1.5 copy-start.12
  94.5 1.5 copy-start.14
  97.0 91.1 %all-gather.9.cloned.1.call-start = ((), (), s32[]{:S(2)}) async-start(), calls=%async_computation.6 | async-start | bytes 1310720 | tf_op jit(solution)/shard_map/all_gather | solution.py:89
  155.4 17.3 %copy-start.3 = (f32[512,256]{1,0:T(8,128)S(1)}, f32[512,256]{1,0:T(8,128)}, u32[]{:S(2)}) copy-start(f32[512,256]{1,0:T(8,128)} %param.17) | copy-start | bytes 1572868
  155.4 17.3 %copy-start.10 = (f32[512,256]{1,0:T(8,128)S(1)}, f32[512,256]{1,0:T(8,128)}, u32[]{:S(2)}) copy-start(f32[512,256]{1,0:T(8,128)} %param.19) | copy-start | bytes 1572868
  155.4 17.3 %copy-start.13 = (f32[256]{0:T(256)S(1)}, f32[256]{0:T(256)}, u32[]{:S(2)}) copy-start(f32[256]{0:T(256)} %param.23) | copy-start | bytes 3076
  200.4 74.3 %all-to-all-start.2 = ((bf16[8,512,256]{2,1,0:T(8,128)(2,1)}), bf16[8,512,256]{2,1,0:T(8,128)(2,1)S(1)}, u32[]{:S(2)}, u32[]{:S(2)}) async-start(bf16[8,512,256]{2,1,0:T(8,128)(2,1)} %bitcast.15), calls=%async_computation.2 | async-start | bytes 4194304 | tf_op jit(solution)/shard_map/all_to_all | solution.py:61
  205.9 120.4 %all-gather.11.cloned.1.call-start = ((), (), s32[]{:S(2)}) async-start(), calls=%async_computation.7 | async-start | bytes 2359296 | tf_op jit(solution)/shard_map/all_gather | solution.py:96
  274.7 1.0 copy-start.5
  274.7 1.2 copy-start.7
  274.8 1.3 copy-start.9
  337.4 17.3 %copy-start.11 = (f32[512,256]{1,0:T(8,128)S(1)}, f32[512,256]{1,0:T(8,128)}, u32[]{:S(2)}) copy-start(f32[512,256]{1,0:T(8,128)} %param.19) | copy-start | bytes 1572868
Sparse Core Ops, SparseCore 0:
  10.1 19.4 all-gather.4
  97.1 47.1 all-gather.6
  173.7 14.3 all-gather.8
  277.3 48.9 all-gather.10

commit v2 on v1

--- a/solution.py
+++ b/solution.py
@@ -7,6 +7,7 @@
 
 NR_DEV = 8
 ZERO_ROWS = 16
+BATCH_PARTS = 2
 
 eps = 1e-06
 
@@ -97,23 +98,29 @@
         partial = jnp.dot(dense, segment, preferred_element_type=jnp.float32)
         return exchange_sum(partial, "col")
 
-    grad_zero = column_sums(y_start)
-    primal_one = jnp.clip(x_start - step_primal * (cost_seg - grad_zero), lower_seg, upper_seg)
-    primal_diff = primal_one - x_start
-    move_primal = jnp.sum(primal_diff * primal_diff, axis=0)
-    image_one = row_sums(2.0 * primal_one - x_start)
-    dual_one = jnp.maximum(y_start + step_dual * (right_side - image_one), 0.0)
-    dual_diff = dual_one - y_start
-    move_dual = jnp.sum(dual_diff * dual_diff, axis=0)
-    moves = lax.psum(jnp.stack([move_primal, move_dual]), ("row", "col"))
-    weight = jnp.sqrt((moves[1] / total_rows + eps) / (moves[0] / total_cols + eps))
-    grad_one = column_sums(dual_one)
-    primal_two = jnp.clip(
-        primal_one - step_primal / weight * (cost_seg - grad_one), lower_seg, upper_seg
-    )
-    image_two = row_sums(2.0 * primal_two - primal_one)
-    dual_out = jnp.maximum(dual_one + step_dual * weight * (right_side - image_two), 0.0)
-    return (primal_two, dual_out)
+    def iterate(x_start, y_start, cost_seg, right_side, lower_seg, upper_seg, step_primal, step_dual):
+        grad_zero = column_sums(y_start)
+        primal_one = jnp.clip(x_start - step_primal * (cost_seg - grad_zero), lower_seg, upper_seg)
+        primal_diff = primal_one - x_start
+        move_primal = jnp.sum(primal_diff * primal_diff, axis=0)
+        image_one = row_sums(2.0 * primal_one - x_start)
+        dual_one = jnp.maximum(y_start + step_dual * (right_side - image_one), 0.0)
+        dual_diff = dual_one - y_start
+        move_dual = jnp.sum(dual_diff * dual_diff, axis=0)
+        moves = lax.psum(jnp.stack([move_primal, move_dual]), ("row", "col"))
+        weight = jnp.sqrt((moves[1] / total_rows + eps) / (moves[0] / total_cols + eps))
+        grad_one = column_sums(dual_one)
+        primal_two = jnp.clip(
+            primal_one - step_primal / weight * (cost_seg - grad_one), lower_seg, upper_seg
+        )
+        image_two = row_sums(2.0 * primal_two - primal_one)
+        dual_out = jnp.maximum(dual_one + step_dual * weight * (right_side - image_two), 0.0)
+        return primal_two, dual_out
+
+    arrays = (x_start, y_start, cost_seg, right_side, lower_seg, upper_seg, step_primal, step_dual)
+    halves = zip(*(jnp.split(array, BATCH_PARTS, axis=-1) for array in arrays))
+    primal_parts, dual_parts = zip(*(iterate(*half) for half in halves))
+    return jnp.concatenate(primal_parts, axis=-1), jnp.concatenate(dual_parts, axis=-1)
 
 
 def solution(mesh):

time: 363 us -> 425 us (1.17)
  blocking collectives: 157 us -> 75.3 us
  waiting for transfers between devices: 116 us -> 194 us
  matrix products: 45.4 us -> 82.2 us
  starting transfers between devices: 5.67 us -> 33 us
    all_to_all x3 -> x0, blocking collectives: 88.1 us -> none  [exchange_sum(): lax.all_to_all(pieces, axis, split_axis=0, concat_axis=0, tiled=True)]
    all_to_all x1 -> x8, waiting for transfers between devices: 0.01 us -> 62.3 us  [exchange_sum(): lax.all_to_all(pieces, axis, split_axis=0, concat_axis=0, tiled=True)]
    all_gather x2 -> x4, waiting for transfers between devices: 96.4 us -> 131 us  [row_sums(): lax.all_gather(ahead.astype(jnp.bfloat16), 'row', axis=0, tiled=True)]
    all_gather x0 -> x4, blocking collectives: none -> 29.4 us  [column_sums(): lax.all_gather(dual.astype(jnp.bfloat16), 'col', axis=0, tiled=True)]
    all_to_all x1 -> x8, starting transfers between devices: 5.52 us -> 32.7 us  [exchange_sum(): lax.all_to_all(pieces, axis, split_axis=0, concat_axis=0, tiled=True)]
    dot_general x2 -> x4, matrix products: 22.1 us -> 45.3 us  [row_sums(): partial = jnp.dot(dense, segment, preferred_element_type=jnp.float32)]
    psum x1, blocking collectives: 68.7 us -> 45.8 us  [iterate(): moves = lax.psum(jnp.stack([move_primal, move_dual]), ('row', 'col'))]
    all_gather x2 -> x0, waiting for transfers between devices: 19 us -> none  [column_sums(): lax.all_gather(dual.astype(jnp.bfloat16), 'col', axis=0, tiled=True)]
  transfers between devices with their start and end apart: 5 -> 12, of which waited for: 4 -> 9; matrix products, arithmetic and copies ran while one was open for 0% -> 15% of each run, Pallas kernels for 3% -> 0%
where the time goes in v2:
time: 425 us; the launch traced here: 424 us
  waiting for transfers between devices  194 us (46%)
  matrix products  82.2 us (19%)
  blocking collectives  75.3 us (18%)
  starting transfers between devices  33 us (8%)
  between operations  14.6 us (3%)
  Pallas kernels  9.62 us (2%)
  other arithmetic  8.31 us (2%)
  local copies, waits for them, and re-layouts  6.99 us (2%)
    all_gather x4, waiting for transfers between devices, row_sums(): lax.all_gather(ahead.astype(jnp.bfloat16), 'row', axis=0, tiled=True)  131 us
    all_to_all x8, waiting for transfers between devices, exchange_sum(): lax.all_to_all(pieces, axis, split_axis=0, concat_axis=0, tiled=True)  62.3 us
    psum x1, blocking collectives, iterate(): moves = lax.psum(jnp.stack([move_primal, move_dual]), ('row', 'col'))  45.8 us
    dot_general x4, matrix products, row_sums(): partial = jnp.dot(dense, segment, preferred_element_type=jnp.float32)  45.3 us
    dot_general x4, matrix products, column_sums(): lax.dot_general(dense, segment, (((0,), (0,)), ((), ())), preferred_eleme...  36.9 us
    all_to_all x8, starting transfers between devices, exchange_sum(): lax.all_to_all(pieces, axis, split_axis=0, concat_axis=0, tiled=True)  32.7 us
    all_gather x4, blocking collectives, column_sums(): lax.all_gather(dual.astype(jnp.bfloat16), 'col', axis=0, tiled=True)  29.4 us
    pallas_call x1, Pallas kernels, lay_out(): pl.pallas_call(lay_out_kernel, out_shape=jax.ShapeDtypeStruct(shape, matr...  9.62 us
  transfers between devices with their start and end apart: 12, of which 9 were waited for; matrix products, arithmetic and copies ran while one was open for 15% of the time, Pallas kernels for 0%

profile of v2, /device:TPU:0, one launch (start us, length us, event | category | flops | bytes accessed | tf_op | source)
XLA Modules:
  0.0 424.3 jit_solution(11580017409171823115)
XLA Ops:
  7.8 1.1 fusion.5
  8.9 8.6 %all_gather.27 = bf16[2048,128]{1,0:T(8,128)(2,1)S(1)} all-gather(bf16[512,128]{1,0:T(8,128)(2,1)S(1)} %get-tuple-element.27), channel_id=1, replica_groups=mesh['row'=8,'col'=4] {'col'}, dimensions={0}, use_global_device_ids=true | all-gather | bytes 655360 | tf_op jit(solution)/shard_map/all_gather | solution.py:90
  17.5 4.6 %copy-done = bf16[1,1,96,256,256]{4,3,2,1,0:T(8,128)(2,1)S(1)} copy-done((bf16[1,1,96,256,256]{4,3,2,1,0:T(8,128)(2,1)S(1)}, bf16[1,1,96,256,256]{4,3,2,1,0:T(8,128)(2,1)}, u32[]{:S(2)}) %copy-start) | copy-done | bytes 12582936
  22.1 0.7 copy-done.1
  22.8 0.7 copy-done.2
  23.4 9.6 %lay_out.1 = bf16[2048,4096]{1,0:T(8,128)(2,1)} custom-call(s32[1,1]{1,0:T(1,128)S(6)} %copy.14.count_ref, s32[1,1,96]{2,1,0:T(1,128)S(1)} %copy-done.1, s32[1,1,96]{2,1,0:T(1,128)S(1)} %copy-done.2, bf16[1,1,96,256,256]{4,3,2,1,0:T(8,128)(2,1)S(1)} %copy-done), custom_call_target="tpu_custom_call" | custom-call | bytes 33554432 | tf_op jit(solution)/shard_map/lay_out/pallas_call | solution.py:45
  33.0 9.3 %convolution_convert_fusion.1 = bf16[4096,128]{1,0:T(8,128)(2,1)} fusion(bf16[2048,4096]{1,0:T(8,128)(2,1)} %lay_out.1, bf16[2048,128]{1,0:T(8,128)(2,1)S(1)} %all_gather.27), kind=kOutput, calls=%fused_computation.1 | convolution fusion | flops 2148007936 | bytes 18350080 | tf_op jit(solution)/shard_map/dot_general | solution.py:91
  42.3 7.5 %all-to-all-start.3 = ((bf16[8,512,128]{2,1,0:T(8,128)(2,1)}), bf16[8,512,128]{2,1,0:T(8,128)(2,1)S(1)}, u32[]{:S(2)}, u32[]{:S(2)}) async-start(bf16[8,512,128]{2,1,0:T(8,128)(2,1)} %bitcast.6), calls=%async_computation.3 | async-start | bytes 2097152 | tf_op jit(solution)/shard_map/all_to_all | solution.py:62
  49.8 7.0 %all_gather.24 = bf16[2048,128]{1,0:T(8,128)(2,1)S(1)} all-gather(bf16[512,128]{1,0:T(8,128)(2,1)S(1)} %get-tuple-element.28), channel_id=1, replica_groups=mesh['row'=8,'col'=4] {'col'}, dimensions={0}, use_global_device_ids=true | all-gather | bytes 655360 | tf_op jit(solution)/shard_map/all_gather | solution.py:90
  56.8 9.2 %convolution_convert_fusion.3 = bf16[4096,128]{1,0:T(8,128)(2,1)} fusion(bf16[2048,4096]{1,0:T(8,128)(2,1)} %lay_out.1, bf16[2048,128]{1,0:T(8,128)(2,1)S(1)} %all_gather.24), kind=kOutput, calls=%fused_computation.3 | convolution fusion | flops 2148007936 | bytes 18350080 | tf_op jit(solution)/shard_map/dot_general | solution.py:91
  66.0 10.1 %all-to-all-done.3 = bf16[8,512,128]{2,1,0:T(8,128)(2,1)S(1)} async-done(((bf16[8,512,128]{2,1,0:T(8,128)(2,1)}), bf16[8,512,128]{2,1,0:T(8,128)(2,1)S(1)}, u32[]{:S(2)}, u32[]{:S(2)}) %all-to-all-start.3) | async-done | bytes 1048608 | tf_op jit(solution)/shard_map/all_to_all | solution.py:62
  76.1 3.6 all-to-all-start
  79.8 0.0 all-gather.5.cloned.1.call-start
  79.8 0.0 copy-done.8
  79.8 0.1 convert_reduce_fusion.1
  80.0 25.7 %all-to-all-done = bf16[8,512,128]{2,1,0:T(8,128)(2,1)S(1)} async-done(((bf16[8,512,128]{2,1,0:T(8,128)(2,1)}), bf16[8,512,128]{2,1,0:T(8,128)(2,1)S(1)}, u32[]{:S(2)}, u32[]{:S(2)}) %all-to-all-start) | async-done | bytes 1048608 | tf_op jit(solution)/shard_map/all_to_all | solution.py:62
  105.7 0.1 convert_reduce_fusion.3
  105.9 0.0 copy-done.4
  105.9 1.5 multiply_reduce_fusion.3
  107.4 1.8 subtract_convert_fusion.2
  109.2 0.0 all-gather.5.cloned.1.call-update
  109.2 0.0 all-gather.7.cloned.1.call-start
  109.2 0.7 all-gather.7.cloned.1.call-update
  110.0 37.8 %all-gather.5.cloned.1.call-done = bf16[4096,128]{1,0:T(8,128)(2,1)} async-done(((bf16[512,128]{1,0:T(8,128)(2,1)}), bf16[4096,128]{1,0:T(8,128)(2,1)}) %all-gather.5.cloned.1.call-update) | async-done | bytes 1048592 | tf_op jit(solution)/shard_map/all_gather | solution.py:97
  147.8 11.3 %convolution_convert_fusion.7 = bf16[2048,128]{1,0:T(8,128)(2,1)} fusion(bf16[2048,4096]{1,0:T(8,128)(2,1)} %lay_out.1, bf16[4096,128]{1,0:T(8,128)(2,1)} %all-gather.5.cloned.1.call-done), kind=kOutput, calls=%fused_computation.7 | convolution fusion | flops 2147745792 | bytes 18350080 | tf_op jit(solution)/shard_map/dot_general | solution.py:98
  159.1 3.8 all-to-all-start.1
  162.9 26.6 %all-gather.7.cloned.1.call-done = bf16[4096,128]{1,0:T(8,128)(2,1)} async-done(((bf16[512,128]{1,0:T(8,128)(2,1)}), bf16[4096,128]{1,0:T(8,128)(2,1)}) %all-gather.7.cloned.1.call-update) | async-done | bytes 1048592 | tf_op jit(solution)/shard_map/all_gather | solution.py:97
  189.5 11.3 %convolution_convert_fusion.6 = bf16[2048,128]{1,0:T(8,128)(2,1)} fusion(bf16[2048,4096]{1,0:T(8,128)(2,1)} %lay_out.1, bf16[4096,128]{1,0:T(8,128)(2,1)} %all-gather.7.cloned.1.call-done), kind=kOutput, calls=%fused_computation.6 | convolution fusion | flops 2147745792 | bytes 18350080 | tf_op jit(solution)/shard_map/dot_general | solution.py:98
  200.8 0.0 all-to-all-done.1
  200.8 3.5 all-to-all-start.4
  204.3 0.1 convert_reduce_fusion.7
  204.4 0.1 fusion.4
  204.5 8.6 %all-to-all-done.4 = bf16[4,512,128]{2,1,0:T(8,128)(2,1)S(1)} async-done(((bf16[4,512,128]{2,1,0:T(8,128)(2,1)}), bf16[4,512,128]{2,1,0:T(8,128)(2,1)S(1)}, u32[]{:S(2)}, u32[]{:S(2)}) %all-to-all-start.4) | async-done | bytes 524320 | tf_op jit(solution)/shard_map/all_to_all | solution.py:62
  213.1 0.1 convert_reduce_fusion.6
  213.1 0.1 multiply_reduce_fusion.2
  213.3 6.5 %all_gather.29 = bf16[2048,128]{1,0:T(8,128)(2,1)S(1)} all-gather(bf16[512,128]{1,0:T(8,128)(2,1)S(1)} %convert_element_type.87), channel_id=1, replica_groups=mesh['row'=8,'col'=4] {'col'}, dimensions={0}, use_global_device_ids=true | all-gather | bytes 655360 | tf_op jit(solution)/shard_map/all_gather | solution.py:90
  219.8 9.2 %convolution_convert_fusion = bf16[4096,128]{1,0:T(8,128)(2,1)} fusion(bf16[2048,4096]{1,0:T(8,128)(2,1)} %lay_out.1, bf16[2048,128]{1,0:T(8,128)(2,1)S(1)} %all_gather.29), kind=kOutput, calls=%fused_computation | convolution fusion | flops 2148007936 | bytes 18350080 | tf_op jit(solution)/shard_map/dot_general | solution.py:91
  229.0 3.6 all-to-all-start.5
  232.6 7.3 %all_gather.26 = bf16[2048,128]{1,0:T(8,128)(2,1)S(1)} all-gather(bf16[512,128]{1,0:T(8,128)(2,1)S(1)} %get-tuple-element.16), channel_id=1, replica_groups=mesh['row'=8,'col'=4] {'col'}, dimensions={0}, use_global_device_ids=true | all-gather | bytes 655360 | tf_op jit(solution)/shard_map/all_gather | solution.py:90
  239.9 9.2 %convolution_convert_fusion.2 = bf16[4096,128]{1,0:T(8,128)(2,1)} fusion(bf16[2048,4096]{1,0:T(8,128)(2,1)} %lay_out.1, bf16[2048,128]{1,0:T(8,128)(2,1)S(1)} %all_gather.26), kind=kOutput, calls=%fused_computation.2 | convolution fusion | flops 2148007936 | bytes 18350080 | tf_op jit(solution)/shard_map/dot_general | solution.py:91
  249.1 10.0 %all-to-all-done.5 = bf16[8,512,128]{2,1,0:T(8,128)(2,1)S(1)} async-done(((bf16[8,512,128]{2,1,0:T(8,128)(2,1)}), bf16[8,512,128]{2,1,0:T(8,128)(2,1)S(1)}, u32[]{:S(2)}, u32[]{:S(2)}) %all-to-all-start.5) | async-done | bytes 1048608 | tf_op jit(solution)/shard_map/all_to_all | solution.py:62
  259.0 3.6 all-to-all-start.2
  262.7 0.0 all-gather.11.cloned.1.call-start
  262.7 45.8 %all-reduce = (f32[2,128]{1,0:T(2,128)S(1)}, f32[2,128]{1,0:T(2,128)S(1)}) all-reduce(f32[2,128]{1,0:T(2,128)S(1)} %get-tuple-element.38, f32[2,128]{1,0:T(2,128)S(1)} %get-tuple-element.37), channel_id=1, replica_groups=mesh['row'=8,'col'=4] {'row','col'}, use_global_device_ids=true, to_apply=%region_10.11 | all-reduce | flops 512 | bytes 4096 | tf_op jit(solution)/shard_map/psum | solution.py:110
  308.6 0.1 convert_reduce_fusion
  308.7 0.0 all-to-all-done.2
  308.8 0.1 convert_reduce_fusion.2
  308.9 2.2 subtract_convert_fusion.1
  311.1 0.0 all-gather.11.cloned.1.call-update
  311.1 0.3 all-gather.9.cloned.1.call-start
  311.4 0.3 all-gather.9.cloned.1.call-update
  311.7 39.9 %all-gather.11.cloned.1.call-done = bf16[4096,128]{1,0:T(8,128)(2,1)} async-done(((bf16[512,128]{1,0:T(8,128)(2,1)}), bf16[4096,128]{1,0:T(8,128)(2,1)}) %all-gather.11.cloned.1.call-update) | async-done | bytes 1048592 | tf_op jit(solution)/shard_map/all_gather | solution.py:97
  351.6 11.3 %convolution_convert_fusion.4 = bf16[2048,128]{1,0:T(8,128)(2,1)} fusion(bf16[2048,4096]{1,0:T(8,128)(2,1)} %lay_out.1, bf16[4096,128]{1,0:T(8,128)(2,1)} %all-gather.11.cloned.1.call-done), kind=kOutput, calls=%fused_computation.4 | convolution fusion | flops 2147745792 | bytes 18350080 | tf_op jit(solution)/shard_map/dot_general | solution.py:98
  362.9 3.6 all-to-all-start.7
  366.6 26.6 %all-gather.9.cloned.1.call-done = bf16[4096,128]{1,0:T(8,128)(2,1)} async-done(((bf16[512,128]{1,0:T(8,128)(2,1)}), bf16[4096,128]{1,0:T(8,128)(2,1)}) %all-gather.9.cloned.1.call-update) | async-done | bytes 1048592 | tf_op jit(solution)/shard_map/all_gather | solution.py:97
  393.2 11.3 %convolution_convert_fusion.5 = bf16[2048,128]{1,0:T(8,128)(2,1)} fusion(bf16[2048,4096]{1,0:T(8,128)(2,1)} %lay_out.1, bf16[4096,128]{1,0:T(8,128)(2,1)} %all-gather.9.cloned.1.call-done), kind=kOutput, calls=%fused_computation.5 | convolution fusion | flops 2147745792 | bytes 18350080 | tf_op jit(solution)/shard_map/dot_general | solution.py:98
  404.5 0.0 all-to-all-done.7
  404.5 3.5 all-to-all-start.6
  408.0 0.8 pad_maximum_fusion
  408.8 0.1 convert_reduce_fusion.4
  408.9 7.9 %all-to-all-done.6 = bf16[4,512,128]{2,1,0:T(8,128)(2,1)S(1)} async-done(((bf16[4,512,128]{2,1,0:T(8,128)(2,1)}), bf16[4,512,128]{2,1,0:T(8,128)(2,1)S(1)}, u32[]{:S(2)}, u32[]{:S(2)}) %all-to-all-start.6) | async-done | bytes 524320 | tf_op jit(solution)/shard_map/all_to_all | solution.py:62
  416.8 0.1 convert_reduce_fusion.5
  416.9 0.1 add_maximum_fusion.1
  416.9 0.8 pad_maximum_fusion.1
  (19 shorter events, 0.1 us)
Async XLA Ops:
  17.5 4.6 %copy-start = (bf16[1,1,96,256,256]{4,3,2,1,0:T(8,128)(2,1)S(1)}, bf16[1,1,96,256,256]{4,3,2,1,0:T(8,128)(2,1)}, u32[]{:S(2)}) copy-start(bf16[1,1,96,256,256]{4,3,2,1,0:T(8,128)(2,1)} %tiles_ref.1) | copy-start | bytes 37748740
  22.1 0.7 copy-start.1
  22.8 0.7 copy-start.2
  42.3 37.5 %copy-start.8 = (f32[256]{0:T(256)S(1)}, f32[256]{0:T(256)}, u32[]{:S(2)}) copy-start(f32[256]{0:T(256)} %param.22) | copy-start | bytes 3076
  42.3 63.6 %copy-start.4 = (f32[512,256]{1,0:T(8,128)S(1)}, f32[512,256]{1,0:T(8,128)}, u32[]{:S(2)}) copy-start(f32[512,256]{1,0:T(8,128)} %param.18) | copy-start | bytes 1572868
  42.3 33.8 %all-to-all-start.3 = ((bf16[8,512,128]{2,1,0:T(8,128)(2,1)}), bf16[8,512,128]{2,1,0:T(8,128)(2,1)S(1)}, u32[]{:S(2)}, u32[]{:S(2)}) async-start(bf16[8,512,128]{2,1,0:T(8,128)(2,1)} %bitcast.6), calls=%async_computation.3 | async-start | bytes 2097152 | tf_op jit(solution)/shard_map/all_to_all | solution.py:62
  76.1 29.6 %all-to-all-start = ((bf16[8,512,128]{2,1,0:T(8,128)(2,1)}), bf16[8,512,128]{2,1,0:T(8,128)(2,1)S(1)}, u32[]{:S(2)}, u32[]{:S(2)}) async-start(bf16[8,512,128]{2,1,0:T(8,128)(2,1)} %bitcast.35), calls=%async_computation | async-start | bytes 2097152 | tf_op jit(solution)/shard_map/all_to_all | solution.py:62
  79.8 68.0 %all-gather.5.cloned.1.call-start = ((), (), s32[]{:S(2)}) async-start(), calls=%async_computation.8 | async-start | bytes 1179648 | tf_op jit(solution)/shard_map/all_gather | solution.py:97
  109.2 80.3 %all-gather.7.cloned.1.call-start = ((), (), s32[]{:S(2)}) async-start(), calls=%async_computation.9 | async-start | bytes 1179648 | tf_op jit(solution)/shard_map/all_gather | solution.py:97
  159.1 45.2 %copy-start.7 = (f32[256]{0:T(256)S(1)}, f32[256]{0:T(256)}, u32[]{:S(2)}) copy-start(f32[256]{0:T(256)} %param.23) | copy-start | bytes 3076
  159.1 45.3 %copy-start.3 = (f32[512,256]{1,0:T(8,128)S(1)}, f32[512,256]{1,0:T(8,128)}, u32[]{:S(2)}) copy-start(f32[512,256]{1,0:T(8,128)} %param.17) | copy-start | bytes 1572868
  159.1 45.3 %copy-start.5 = (f32[512,256]{1,0:T(8,128)S(1)}, f32[512,256]{1,0:T(8,128)}, u32[]{:S(2)}) copy-start(f32[512,256]{1,0:T(8,128)} %param.19) | copy-start | bytes 1572868
  159.1 41.7 %all-to-all-start.1 = ((bf16[4,512,128]{2,1,0:T(8,128)(2,1)}), bf16[4,512,128]{2,1,0:T(8,128)(2,1)S(1)}, u32[]{:S(2)}, u32[]{:S(2)}) async-start(bf16[4,512,128]{2,1,0:T(8,128)(2,1)} %bitcast.2), calls=%async_computation.1 | async-start | bytes 1048576 | tf_op jit(solution)/shard_map/all_to_all | solution.py:62
  200.8 12.3 %all-to-all-start.4 = ((bf16[4,512,128]{2,1,0:T(8,128)(2,1)}), bf16[4,512,128]{2,1,0:T(8,128)(2,1)S(1)}, u32[]{:S(2)}, u32[]{:S(2)}) async-start(bf16[4,512,128]{2,1,0:T(8,128)(2,1)} %bitcast.36), calls=%async_computation.4 | async-start | bytes 1048576 | tf_op jit(solution)/shard_map/all_to_all | solution.py:62
  229.0 30.0 %all-to-all-start.5 = ((bf16[8,512,128]{2,1,0:T(8,128)(2,1)}), bf16[8,512,128]{2,1,0:T(8,128)(2,1)S(1)}, u32[]{:S(2)}, u32[]{:S(2)}) async-start(bf16[8,512,128]{2,1,0:T(8,128)(2,1)} %bitcast.11), calls=%async_computation.5 | async-start | bytes 2097152 | tf_op jit(solution)/shard_map/all_to_all | solution.py:62
  259.0 49.7 %all-to-all-start.2 = ((bf16[8,512,128]{2,1,0:T(8,128)(2,1)}), bf16[8,512,128]{2,1,0:T(8,128)(2,1)S(1)}, u32[]{:S(2)}, u32[]{:S(2)}) async-start(bf16[8,512,128]{2,1,0:T(8,128)(2,1)} %bitcast.34), calls=%async_computation.2 | async-start | bytes 2097152 | tf_op jit(solution)/shard_map/all_to_all | solution.py:62
  262.7 88.9 %all-gather.11.cloned.1.call-start = ((), (), s32[]{:S(2)}) async-start(), calls=%async_computation.11 | async-start | bytes 1179648 | tf_op jit(solution)/shard_map/all_gather | solution.py:97
  311.1 82.1 %all-gather.9.cloned.1.call-start = ((), (), s32[]{:S(2)}) async-start(), calls=%async_computation.10 | async-start | bytes 1179648 | tf_op jit(solution)/shard_map/all_gather | solution.py:97
  362.9 53.9 %copy-start.6 = (f32[512,256]{1,0:T(8,128)S(1)}, f32[512,256]{1,0:T(8,128)}, u32[]{:S(2)}) copy-start(f32[512,256]{1,0:T(8,128)} %param.19) | copy-start | bytes 1572868
  362.9 41.6 %all-to-all-start.7 = ((bf16[4,512,128]{2,1,0:T(8,128)(2,1)}), bf16[4,512,128]{2,1,0:T(8,128)(2,1)S(1)}, u32[]{:S(2)}, u32[]{:S(2)}) async-start(bf16[4,512,128]{2,1,0:T(8,128)(2,1)} %bitcast.13), calls=%async_computation.7 | async-start | bytes 1048576 | tf_op jit(solution)/shard_map/all_to_all | solution.py:62
  404.5 12.3 %all-to-all-start.6 = ((bf16[4,512,128]{2,1,0:T(8,128)(2,1)}), bf16[4,512,128]{2,1,0:T(8,128)(2,1)S(1)}, u32[]{:S(2)}, u32[]{:S(2)}) async-start(bf16[4,512,128]{2,1,0:T(8,128)(2,1)} %bitcast.12), calls=%async_computation.6 | async-start | bytes 1048576 | tf_op jit(solution)/shard_map/all_to_all | solution.py:62
Sparse Core Ops, SparseCore 0:
  109.3 38.3 all-gather.4
  150.5 38.9 all-gather.6
  311.2 40.3 all-gather.10
  354.2 38.9 all-gather.8
